TPU v7x, 256 devices: a whole 4x4x8 slice. The times are simulated.
256 devices in a mesh: seq: 32 (over x, z), tensor: 8 (over y, core).
Axes of the slice: x: 4, y: 4, z: 8, core: 2. Of those that a mesh axis runs over, the one named last changes fastest.
Arguments:
- hidden_in: bfloat16 [12288, 4096], P('seq', 'tensor'), may hold values from -6 to 6
- norm_gain: float32 [4096], replicated, may hold values from 0.5 to 1.5
- w_x: bfloat16 [4096, 8192], P('seq', 'tensor'), may hold values from -0.09375 to 0.09375
- w_z: bfloat16 [4096, 8192], P('seq', 'tensor'), may hold values from -0.09375 to 0.09375
- w_bc: bfloat16 [4096, 8, 256], P('seq', 'tensor'), may hold values from -0.09375 to 0.09375
- w_dt: bfloat16 [4096, 64], P('seq', 'tensor'), may hold values from -0.09375 to 0.09375
- dt_bias: float32 [64], P('tensor'), may hold values from -6 to -2
- decay_rate: float32 [64], P('tensor'), may hold values from 8.138021e-05 to 8
- conv_x: float32 [4, 8192], P(None, 'tensor'), may hold values from -3 to 3
- conv_bc: float32 [4, 8, 256], P(None, 'tensor'), may hold values from -3 to 3
- conv_bias_x: float32 [8192], P('tensor'), may hold values from -3 to 3
- conv_bias_bc: float32 [8, 256], P('tensor'), may hold values from -3 to 3
- skip_d: float32 [64], P('tensor'), may hold values from 0.5 to 8
- out_gain: float32 [8192], P('tensor'), may hold values from 0.5 to 1.5
- w_out: bfloat16 [8192, 4096], P('tensor'), may hold values from -0.0625 to 0.0625
Outputs:
- layer_out: bfloat16 [12288, 4096], P('seq', 'tensor')
All inputs are finite; a program needn't handle non-finite values.
Results may differ from a plain program's by a relative error of at most 0.0095.
Values may be sent and summed in bfloat16 or wider, within the bound.
No kernel may reach another device: no remote copies, remote signals or barrier semaphores. Data moves between devices by JAX's collectives and lax.ppermute only.
A program may use at most 128 MiB of HBM per device.

v0:
```python
import math
import jax
import jax.numpy as jnp
from jax import lax
from jax.sharding import Mesh
from jax.sharding import PartitionSpec as P

SPAN = 128
SEQ = ("seq_0", "seq_1")
epsilon = 1e-05


def side_by_side(arrays, axis, dim, along):
    widths = [math.prod(a.shape[along:]) for a in arrays]
    both = jnp.concatenate(
        [a.reshape(*a.shape[:along], w) for a, w in zip(arrays, widths)], axis=along
    )
    whole = lax.all_gather(both, axis, axis=dim, tiled=True)
    tiles = jnp.split(whole, [sum(widths[:k]) for k in range(1, len(widths))], axis=along)
    return tuple((b.reshape(*whole.shape[:along], *a.shape[along:]) for a, b in zip(arrays, tiles)))


def passed_along(block, axis, distance):
    devices = range(lax.axis_size(axis))
    route = [(i - distance, i) for i in devices if i - distance in devices]
    return lax.ppermute(block, axis, route)


def nothing_yet(array, identity):
    return jax.tree.map(
        lambda a, e: jnp.broadcast_to(jnp.asarray(e, a.dtype), a.shape), array, identity
    )


def entering(array, axes, combine, identity):
    before = start = nothing_yet(array, identity)
    running = array
    for axis in reversed(axes):
        peers, place = (lax.axis_size(axis), lax.axis_index(axis))
        pieces = jax.tree.map(lambda part: lax.all_gather(part, axis), running)
        inside, running = (start, start)
        for k in range(peers):
            passed = k < place
            running = combine(running, jax.tree.map(lambda part: part[k], pieces))
            inside = jax.tree.map(lambda new, old: jnp.where(passed, new, old), running, inside)
        before = combine(inside, before)
    return before


def rms_scale(values, norm_weight):
    return (
        values
        * lax.rsqrt(jnp.mean(values * values, axis=-1, keepdims=True) + epsilon)
        * norm_weight
    )


def causal_conv(padded, weight, bias_row):
    tap_count = weight.shape[0]
    out_length = padded.shape[0] - tap_count + 1
    running = bias_row
    for k in range(tap_count):
        running = running + weight[k] * padded[k : k + out_length].astype(jnp.float32)
    return jax.nn.silu(running).astype(jnp.bfloat16)


def span_terms(x_blocks, b_blocks, c_blocks, log_decay, dt_blocks):
    cum_decay = jnp.cumsum(log_decay, axis=1)
    scores = jnp.einsum("ctgn,csgn->cgts", c_blocks, b_blocks, preferred_element_type=jnp.float32)
    length = x_blocks.shape[1]
    causal_mask = lax.broadcasted_iota(jnp.int32, (length, length), 0) >= lax.broadcasted_iota(
        jnp.int32, (length, length), 1
    )
    cum_rows = jnp.transpose(cum_decay, (0, 2, 3, 1))
    decay_gap = cum_rows[..., :, None] - cum_rows[..., None, :]
    decay_mat = jnp.where(causal_mask, jnp.exp(jnp.where(causal_mask, decay_gap, 0.0)), 0.0)
    dt_cols = jnp.transpose(dt_blocks, (0, 2, 3, 1))[..., None, :]
    mix_weight = (scores[:, :, None] * decay_mat * dt_cols).astype(jnp.bfloat16)
    intra_out = jnp.einsum(
        "cgkts,csgkp->ctgkp", mix_weight, x_blocks, preferred_element_type=jnp.float32
    )
    tail_decay = jnp.exp(cum_decay[:, -1:] - cum_decay) * dt_blocks
    scaled = (x_blocks.astype(jnp.float32) * tail_decay[..., None]).astype(jnp.bfloat16)
    fresh_state = jnp.einsum(
        "csgkp,csgn->cgkpn", scaled, b_blocks, preferred_element_type=jnp.float32
    )
    return (cum_decay, intra_out, fresh_state)


def combine(first_part, second_part):
    return (
        first_part[0] * second_part[0],
        second_part[0][..., None, None] * first_part[1] + second_part[1],
    )


def local(
    hidden_in,
    norm_gain,
    w_x,
    w_z,
    w_bc,
    w_dt,
    dt_bias,
    decay_rate,
    conv_x,
    conv_bc,
    conv_bias_x,
    conv_bias_bc,
    skip_d,
    out_gain,
    w_out,
):
    gathered = lax.all_gather(hidden_in, "tensor", axis=1, tiled=True)
    normed = rms_scale(gathered.astype(jnp.float32), norm_gain).astype(jnp.bfloat16)
    row_count = normed.shape[0]
    rim_rows = conv_x.shape[0] - 1
    groups = w_bc.shape[1]
    bc_width = w_bc.shape[2]
    state_dim = bc_width // 2
    head_count = decay_rate.shape[0]
    inner_width = w_x.shape[1]
    head_dim = inner_width // head_count
    per_group = head_count // groups
    full_x, full_z, full_bc, full_dt = side_by_side((w_x, w_z, w_bc, w_dt), SEQ, 0, 1)
    proj_x = jnp.dot(normed, full_x, preferred_element_type=jnp.float32)
    gate_z = jnp.dot(normed, full_z, preferred_element_type=jnp.float32)
    proj_bc = jnp.dot(
        normed,
        full_bc.reshape(full_bc.shape[0], groups * bc_width),
        preferred_element_type=jnp.float32,
    )
    dt_raw = jnp.dot(normed, full_dt, preferred_element_type=jnp.float32)
    proj_x = proj_x.astype(jnp.bfloat16)
    proj_bc = proj_bc.astype(jnp.bfloat16).reshape(row_count, groups, bc_width)
    edge_x, edge_bc = passed_along(
        (proj_x[row_count - rim_rows :], proj_bc[row_count - rim_rows :]), SEQ, 1
    )
    padded_x = jnp.concatenate([edge_x, proj_x], axis=0)
    padded_bc = jnp.concatenate([edge_bc, proj_bc], axis=0)
    gate_z = gate_z.astype(jnp.bfloat16)
    dt_vals = jax.nn.softplus(dt_raw + dt_bias)
    x_conv = causal_conv(padded_x, conv_x, conv_bias_x)
    bc_conv = causal_conv(padded_bc, conv_bc, conv_bias_bc)
    span_count = row_count // SPAN
    x_blocks = x_conv.reshape(span_count, SPAN, groups, per_group, head_dim)
    b_blocks = bc_conv[..., :state_dim].reshape(span_count, SPAN, groups, state_dim)
    c_blocks = bc_conv[..., state_dim:].reshape(span_count, SPAN, groups, state_dim)
    log_decay = (-dt_vals * decay_rate).reshape(span_count, SPAN, groups, per_group)
    dt_blocks = dt_vals.reshape(span_count, SPAN, groups, per_group)
    cum_decay, intra_out, fresh_state = span_terms(
        x_blocks, b_blocks, c_blocks, log_decay, dt_blocks
    )
    block_totals = cum_decay[:, -1]

    def carry_step(state_in, block_item):
        log_total, block_state = block_item
        return (jnp.exp(log_total)[..., None, None] * state_in + block_state, state_in)

    start_state = jnp.zeros((groups, per_group, head_dim, state_dim), jnp.float32)
    local_final, local_enter = lax.scan(carry_step, start_state, (block_totals, fresh_state))
    before_log = jnp.cumsum(block_totals, axis=0) - block_totals
    device_decay = jnp.exp(jnp.sum(block_totals, axis=0))
    identity = (jnp.ones_like(device_decay), jnp.zeros_like(local_final))
    c_float = c_blocks.astype(jnp.float32)
    incoming = entering((device_decay, local_final), SEQ, combine, identity)[1]
    enter_state = local_enter + jnp.exp(before_log)[..., None, None] * incoming[None]
    inter_out = jnp.exp(cum_decay)[..., None] * jnp.einsum(
        "ctgn,cgkpn->ctgkp", c_float, enter_state
    )
    skip_heads = skip_d.reshape(groups, per_group)[..., None]
    ssm_out = (intra_out + inter_out + skip_heads * x_blocks.astype(jnp.float32)).reshape(
        row_count, inner_width
    )
    gated_out = ssm_out * jax.nn.silu(gate_z.astype(jnp.float32))
    grouped = gated_out.reshape(row_count, groups, inner_width // groups)
    normed_y = (
        rms_scale(grouped, out_gain.reshape(groups, inner_width // groups))
        .reshape(row_count, inner_width)
        .astype(jnp.bfloat16)
    )
    partial_value = jnp.dot(normed_y, w_out, preferred_element_type=jnp.float32)
    summed = lax.psum_scatter(partial_value, "tensor", scatter_dimension=1, tiled=True)
    return (hidden_in.astype(jnp.float32) + summed).astype(jnp.bfloat16)


def solution(mesh):
    split = Mesh(mesh.devices.reshape(4, 8, mesh.shape["tensor"]), ("seq_0", "seq_1", "tensor"))
    in_specs = (
        P(SEQ, "tensor"),
        P(),
        P(SEQ, "tensor"),
        P(SEQ, "tensor"),
        P(SEQ, "tensor", None),
        P(SEQ, "tensor"),
        P("tensor"),
        P("tensor"),
        P(None, "tensor"),
        P(None, "tensor", None),
        P("tensor"),
        P("tensor", None),
        P("tensor"),
        P("tensor"),
        P("tensor", None),
    )
    out_specs = P(SEQ, "tensor")
    return jax.shard_map(local, mesh=split, in_specs=in_specs, out_specs=out_specs, check_vma=False)
```

profile of v0, /device:TPU:1, one launch (start us, length us, event | category | flops | bytes accessed | tf_op | source)
XLA Modules:
  0.0 395.8 jit_solution(16291231252548557750)
XLA Ops:
  6.5 0.7 all-gather.7.cloned.1.call-update
  7.3 0.8 copy.40
  8.1 2.0 pad_maximum_fusion.1
  10.2 33.4 %all-gather.7.cloned.1.call-done = bf16[384,4096]{1,0:T(8,128)(2,1)} async-done(((bf16[384,512]{1,0:T(8,128)(2,1)}), bf16[384,4096]{1,0:T(8,128)(2,1)}) %all-gather.7.cloned.1.call-update) | async-done | bytes 3145744 | tf_op jit(solution)/shard_map/all_gather | solution.py:114
  43.7 2.6 fusion.6
  46.3 154.4 %all-gather.9.cloned.1.call-done = bf16[4096,2312]{1,0:T(8,128)(2,1)} async-done(((bf16[128,2312]{1,0:T(8,128)(2,1)}), bf16[4096,2312]{1,0:T(8,128)(2,1)}) %all-gather.9.cloned.1.call-update) | async-done | bytes 18939920 | tf_op jit(solution)/shard_map/all_gather | solution.py:18
  200.7 3.2 compare_select_fusion
  204.3 3.7 fusion.29
  208.1 1.4 collective-permute-start.1
  209.6 6.9 %fusion.23 = bf16[384,1024]{1,0:T(8,128)(2,1)S(1)} fusion(bf16[4096,2312]{1,0:T(8,128)(2,1)} %all-gather.9.cloned.1.call-done, bf16[384,4096]{1,0:T(8,128)(2,1)S(1)} %copy-done.3, f32[4096]{0:T(1024)S(1)} %copy-done.15, f32[384]{0:T(512)S(1)} %add_rsqrt_fusion.1), kind=kOutput, calls=%fused_computation.36 | convolution fusion | flops 3227910144 | bytes 12338688 | tf_op jit(solution)/shard_map/dot_general | solution.py:126
  216.5 3.2 collective-permute-start
  220.5 2.2 convert_bitcast_fusion
  224.4 3.0 while.13
  224.4 0.8 bitcast_dynamic-update-slice_fusion.2
  225.4 0.9 bitcast_dynamic-update-slice_fusion.2
  226.4 0.8 bitcast_dynamic-update-slice_fusion.2
  227.3 0.8 copy-done
  228.2 0.6 dynamic-slice
  229.6 14.0 %all-reduce = f32[64]{0:T(128)S(1)} all-reduce(f32[64]{0:T(128)S(1)} %exponential_dynamic-update-slice_fusion), channel_id=2, replica_groups=mesh['seq_0'=4,'seq_1'=8,'tensor'=8] {'seq_1'}, use_global_device_ids=true, to_apply=%add | all-reduce | flops 64 | bytes 512
  243.8 41.7 %all-gather.13.cloned.1.call-done = f32[8,8,128,128]{3,2,1,0:T(8,128)} async-done(((f32[1,8,128,128]{3,2,1,0:T(8,128)}), f32[8,8,128,128]{3,2,1,0:T(8,128)}) %all-gather.13.cloned.1.call-update) | async-done | bytes 4194320 | tf_op jit(solution)/shard_map/all_gather | solution.py:40
  285.5 3.5 fusion.54
  289.1 7.7 %all_gather.27 = f32[4,1,8]{2,1,0:T(1,128)S(1)} all-gather(f32[1,1,8]{2,1,0:T(1,128)S(1)} %get-tuple-element.105), channel_id=1, replica_groups=mesh['seq_0'=4,'seq_1'=8,'tensor'=8] {'seq_0'}, dimensions={0}, use_global_device_ids=true | all-gather | bytes 160 | tf_op jit(solution)/shard_map/all_gather | solution.py:40
  297.0 0.9 fusion.78
  298.8 3.2 fusion.35
  302.0 19.0 %all-gather.11.cloned.1.call-done = f32[4,1,8,128,128]{4,3,2,1,0:T(8,128)} async-done(((f32[1,1,8,128,128]{4,3,2,1,0:T(8,128)}), f32[4,1,8,128,128]{4,3,2,1,0:T(8,128)}) %all-gather.11.cloned.1.call-update) | async-done | bytes 2097168 | tf_op jit(solution)/shard_map/all_gather | solution.py:40
  321.0 3.7 fusion.53
  324.8 0.5 fusion.16
  325.4 0.6 copy.49
  326.1 7.4 %multiply_reduce_fusion = (f32[384]{0:T(512)S(1)}, f32[384,1024]{1,0:T(8,128)S(1)}) fusion(bf16[4096,2312]{1,0:T(8,128)(2,1)} %all-gather.9.cloned.1.call-done, bf16[384,4096]{1,0:T(8,128)(2,1)} %all-gather.7.cloned.1.call-done, f32[4096]{0:T(1024)S(1)} %copy-done.16, f32[384]{0:T(512)S(1)} %add_rsqrt_fusion.1, f32[48,8,8,128]{3,2,1,0:T(8,128)S(1)} %bitcast.191), kind=kOutput, calls=%fused_computation.29 | convolution fusion | flops 3231055360 | bytes 14699520 | tf_op jit(solution)/shard_map/dot_general | solution.py:127
  333.5 8.8 %fusion.38 = f32[384,4096]{1,0:T(8,128)} fusion(bf16[1024,4096]{1,0:T(8,128)(2,1)} %param.31, f32[384,1024]{1,0:T(8,128)S(1)} %get-tuple-element.112, f32[1024]{0:T(1024)S(1)} %copy-done.17, f32[384]{0:T(512)S(1)} %add_rsqrt_fusion), kind=kOutput, calls=%fused_computation.46 | convolution fusion | flops 3222405120 | bytes 16258560 | tf_op jit(solution)/shard_map/dot_general | solution.py:182
  342.4 44.9 %reduce-scatter.2.cloned.1.call-done = f32[384,512]{1,0:T(8,128)} async-done(((f32[384,4096]{1,0:T(8,128)}), f32[384,512]{1,0:T(8,128)}) %reduce-scatter.2.cloned.1.call-update) | async-done | bytes 786448 | tf_op jit(solution)/shard_map/reduce_scatter | solution.py:183
  387.3 2.0 add_convert_fusion
  (87 shorter events, 4.9 us)
Async XLA Ops:
  6.5 3.6 copy-start.11
  6.5 3.6 copy-start.9
  6.5 37.1 %all-gather.7.cloned.1.call-start = ((), (), s32[]{:S(2)}) async-start(), calls=%async_computation.1 | async-start | bytes 3538944 | tf_op jit(solution)/shard_map/all_gather | solution.py:114
  7.3 193.4 %all-gather.9.cloned.1.call-start = ((), (), s32[]{:S(2)}) async-start(), calls=%async_computation.2 | async-start | bytes 20545536 | tf_op jit(solution)/shard_map/all_gather | solution.py:18
  10.1 275.4 %all-gather.13.cloned.1.call-start = ((), (), s32[]{:S(2)}) async-start(), calls=%async_computation.5 | async-start | bytes 4718592 | tf_op jit(solution)/shard_map/all_gather | solution.py:40
  10.2 190.4 %copy-start.15 = (f32[4096]{0:T(1024)S(1)}, f32[4096]{0:T(1024)}, u32[]{:S(2)}) copy-start(f32[4096]{0:T(1024)} %param.18) | copy-start | bytes 49156
  10.2 190.4 %copy-start.18 = (f32[8]{0:T(128)S(1)}, f32[8]{0:T(128)}, u32[]{:S(2)}) copy-start(f32[8]{0:T(128)} %param.23) | copy-start | bytes 100
  46.3 157.6 %copy-start.14 = (f32[8]{0:T(128)S(1)}, f32[8]{0:T(128)}, u32[]{:S(2)}) copy-start(f32[8]{0:T(128)} %param.24) | copy-start | bytes 100
  204.3 5.2 %copy-start.3 = (bf16[384,4096]{1,0:T(8,128)(2,1)S(1)}, bf16[384,4096]{1,0:T(8,128)(2,1)}, u32[]{:S(2)}) copy-start(bf16[384,4096]{1,0:T(8,128)(2,1)} %all-gather.7.cloned.1.call-done) | copy-start | bytes 9437188
  208.1 11.7 %collective-permute-start.1 = (bf16[3,1,256]{2,0,1:T(4,128)(2,1)S(1)}, bf16[3,1,256]{2,0,1:T(4,128)(2,1)S(1)}, u32[]{:S(2)}, u32[]{:S(2)}) collective-permute-start(bf16[3,1,256]{2,0,1:T(4,128)(2,1)S(1)} %slice_bitcast_fusion.8), channel_id=1, source_target_pairs={{0,8},{8,16},{16,24},{24,32},{32,40},{40,48},{48,56},{56,64},{64,7... | collective-permute-start | bytes 4616 | tf_op jit(solution)/shard_map/ppermute | solution.py:26
  209.6 10.3 %copy-start.12 = (f32[1,256]{1,0:T(1,128)S(1)}, f32[1,256]{1,0:T(1,128)}, u32[]{:S(2)}) copy-start(f32[1,256]{1,0:T(1,128)} %param.28) | copy-start | bytes 3076
  209.6 10.9 %copy-start.10 = (f32[1024]{0:T(1024)S(1)}, f32[1024]{0:T(1024)}, u32[]{:S(2)}) copy-start(f32[1024]{0:T(1024)} %param.27) | copy-start | bytes 12292
  216.5 4.0 %collective-permute-start = (bf16[3,1024]{1,0:T(4,128)(2,1)S(1)}, bf16[3,1024]{1,0:T(4,128)(2,1)S(1)}, u32[]{:S(2)}, u32[]{:S(2)}) collective-permute-start(bf16[3,1024]{1,0:T(4,128)(2,1)S(1)} %slice.193), channel_id=1, source_target_pairs={{0,8},{8,16},{16,24},{24,32},{32,40},{40,48},{48,56},{56,64},{64,7... | collective-permute-start | bytes 18440 | tf_op jit(solution)/shard_map/ppermute | solution.py:26
  223.5 0.9 copy-start.4
  223.8 4.4 %copy-start.19 = (u32[256]{0:T(256)S(1)}, u32[256]{0:T(256)}, u32[]{:S(2)}) copy-start(u32[256]{0:T(256)} %constant.70) | copy-start | bytes 3076
  227.3 0.8 copy-start
  228.2 92.8 %all-gather.11.cloned.1.call-start = ((), (), s32[]{:S(2)}) async-start(), calls=%async_computation.3 | async-start | bytes 2621440 | tf_op jit(solution)/shard_map/all_gather | solution.py:40
  285.5 12.4 %copy-start.1 = (f32[48,8,8,128]{3,1,2,0:T(8,128)S(1)}, f32[48,8,8,128]{3,1,2,0:T(8,128)}, u32[]{:S(2)}) copy-start(f32[48,8,8,128]{3,1,2,0:T(8,128)} %get-tuple-element.80) | copy-start | bytes 4718596
  289.1 98.2 %reduce-scatter.2.cloned.1.call-start = ((), (), s32[]{:S(2)}) async-start(), calls=%async_computation.4 | async-start | bytes 7077888 | tf_op jit(solution)/shard_map/reduce_scatter | solution.py:183
  298.7 22.2 %copy-start.2 = (f32[1,1,8,128,128]{4,3,2,1,0:T(8,128)S(1)}, f32[1,1,8,128,128]{4,3,2,1,0:T(8,128)}, u32[]{:S(2)}) copy-start(f32[1,1,8,128,128]{4,3,2,1,0:T(8,128)} %get-tuple-element.78) | copy-start | bytes 1572868
  298.8 22.2 %copy-start.5 = (f32[1,1,8,128,128]{4,3,2,1,0:T(8,128)S(1)}, f32[1,1,8,128,128]{4,3,2,1,0:T(8,128)}, u32[]{:S(2)}) copy-start(f32[1,1,8,128,128]{4,3,2,1,0:T(8,128)} %get-tuple-element.79) | copy-start | bytes 1572868
  321.0 3.8 copy-start.7
  321.0 3.8 copy-start.8
  321.0 3.8 copy-start.13
  325.3 0.7 copy-start.16
  326.1 7.5 %copy-start.17 = (f32[1024]{0:T(1024)S(1)}, f32[1024]{0:T(1024)}, u32[]{:S(2)}) copy-start(f32[1024]{0:T(1024)} %param.30) | copy-start | bytes 12292
  342.4 44.9 %copy-start.6 = (bf16[384,512]{1,0:T(8,128)(2,1)S(1)}, bf16[384,512]{1,0:T(8,128)(2,1)}, u32[]{:S(2)}) copy-start(bf16[384,512]{1,0:T(8,128)(2,1)} %param.17) | copy-start | bytes 1179652
Sparse Core Ops, SparseCore 0:
  9.2 34.4 all-gather.6
  46.2 154.3 all-gather.8
  228.3 57.1 all-gather.12
  289.2 31.7 all-gather.10
  342.5 44.7 reduce-scatter.1
where the time goes:
time: 396 us
  waiting for transfers between devices  295 us (74%)
  matrix products  35.2 us (9%)
  blocking collectives  21.8 us (6%)
  other arithmetic  19.8 us (5%)
  between operations  14.2 us (4%)
  local copies, waits for them, and re-layouts  5.45 us (1%)
  starting transfers between devices  4.78 us (1%)
    all_gather x1, waiting for transfers between devices, side_by_side(): whole = lax.all_gather(both, axis, axis=dim, tiled=True)  154 us
    all_gather x2, waiting for transfers between devices, entering(): pieces = jax.tree.map(lambda part: lax.all_gather(part, axis), running)  60.7 us
    reduce_scatter x1, waiting for transfers between devices, local(): lax.psum_scatter(partial_value, 'tensor', scatter_dimension=1, tiled=True)  44.9 us
    all_gather x1, waiting for transfers between devices, local(): gathered = lax.all_gather(hidden_in, 'tensor', axis=1, tiled=True)  33.4 us
    unnamed x1, blocking collectives  14 us
    dot_general x1, matrix products, local(): partial_value = jnp.dot(normed_y, w_out, preferred_element_type=jnp.float32)  8.85 us
  transfers between devices with their start and end apart: 7, of which 6 were waited for; matrix products, arithmetic and copies ran while one was open for 5% of the time, Pallas kernels for 0%

commit v1 on v0

--- a/solution.py
+++ b/solution.py
@@ -8,6 +8,27 @@
 SPAN = 128
 SEQ = ("seq_0", "seq_1")
 epsilon = 1e-05
+
+
+def prepare_the_panel(array_here, array_axis):
+    part_next = list(array_here.shape[1:])
+    part_next[array_axis] *= array_here.shape[0]
+    return jnp.moveaxis(array_here, 0, array_axis).reshape(part_next)
+
+
+def wrap_local_data_up(xin, bus_axis):
+    a_next = lax.axis_size(bus_axis)
+    outer, block_now = (a_next, lax.axis_index(bus_axis))
+    reply, p_next = (xin[None], 1)
+    while p_next < outer:
+        column = []
+        for q in range(outer):
+            column.append((q, q ^ p_next))
+        odd = lax.ppermute(reply, bus_axis, column)
+        a_now = block_now & p_next == 0
+        reply = jnp.concatenate([jnp.where(a_now, reply, odd), jnp.where(a_now, odd, reply)])
+        p_next *= 2
+    return reply
 
 
 def side_by_side(arrays, axis, dim, along):
@@ -111,7 +132,8 @@
     out_gain,
     w_out,
 ):
-    gathered = lax.all_gather(hidden_in, "tensor", axis=1, tiled=True)
+    h_now = wrap_local_data_up(hidden_in, "tensor")
+    gathered = prepare_the_panel(h_now, 1)
     normed = rms_scale(gathered.astype(jnp.float32), norm_gain).astype(jnp.bfloat16)
     row_count = normed.shape[0]
     rim_rows = conv_x.shape[0] - 1

time: 396 us -> 368 us (0.929)
  waiting for transfers between devices: 295 us -> 249 us
  other arithmetic: 19.8 us -> 28.3 us
  starting transfers between devices: 4.78 us -> 9.3 us
  local copies, waits for them, and re-layouts: 5.45 us -> 9.42 us
    all_gather x1, waiting for transfers between devices: 154 us -> 90.1 us  [side_by_side(): whole = lax.all_gather(both, axis, axis=dim, tiled=True)]
    ppermute x0 -> x3, waiting for transfers between devices: none -> 55.5 us  [wrap_local_data_up(): odd = lax.ppermute(reply, bus_axis, column)]
    all_gather x1 -> x0, waiting for transfers between devices: 33.4 us -> none  [local(): gathered = lax.all_gather(hidden_in, 'tensor', axis=1, tiled=True)]
    ppermute x0 -> x3, starting transfers between devices: none -> 4.57 us  [wrap_local_data_up(): odd = lax.ppermute(reply, bus_axis, column)]
  transfers between devices with their start and end apart: 7 -> 9, of which waited for: 6 -> 7; matrix products, arithmetic and copies ran while one was open for 5% -> 7% of each run, Pallas kernels for 0% -> 0%
where the time goes in v1:
time: 368 us
  waiting for transfers between devices  249 us (68%)
  matrix products  36.5 us (10%)
  other arithmetic  28.3 us (8%)
  blocking collectives  20.9 us (6%)
  between operations  14.5 us (4%)
  local copies, waits for them, and re-layouts  9.42 us (3%)
  starting transfers between devices  9.3 us (3%)
    all_gather x1, waiting for transfers between devices, side_by_side(): whole = lax.all_gather(both, axis, axis=dim, tiled=True)  90.1 us
    all_gather x2, waiting for transfers between devices, entering(): pieces = jax.tree.map(lambda part: lax.all_gather(part, axis), running)  58.1 us
    ppermute x3, waiting for transfers between devices, wrap_local_data_up(): odd = lax.ppermute(reply, bus_axis, column)  55.5 us
    reduce_scatter x1, waiting for transfers between devices, local(): lax.psum_scatter(partial_value, 'tensor', scatter_dimension=1, tiled=True)  44.9 us
    unnamed x1, blocking collectives  13.2 us
    dot_general x1, matrix products, local(): partial_value = jnp.dot(normed_y, w_out, preferred_element_type=jnp.float32)  8.82 us
    dot_general x1, matrix products, local(): gate_z = jnp.dot(normed, full_z, preferred_element_type=jnp.float32)  7.89 us
    all_gather x1, blocking collectives, entering(): pieces = jax.tree.map(lambda part: lax.all_gather(part, axis), running)  7.72 us
  transfers between devices with their start and end apart: 9, of which 7 were waited for; matrix products, arithmetic and copies ran while one was open for 7% of the time, Pallas kernels for 0%

profile of v1, /device:TPU:1, one launch (start us, length us, event | category | flops | bytes accessed | tf_op | source)
XLA Modules:
  0.0 367.6 jit_solution(7176093356508618887)
XLA Ops:
  7.4 1.9 pad_maximum_fusion.3
  9.6 3.3 collective-permute-start
  12.9 1.3 collective-permute-done
  14.6 18.8 %collective-permute-done.1 = bf16[2,384,512]{1,2,0:T(8,128)(2,1)} collective-permute-done((bf16[2,384,512]{1,2,0:T(8,128)(2,1)S(1)}, bf16[2,384,512]{1,2,0:T(8,128)(2,1)}, u32[]{:S(2)}, u32[]{:S(2)}) %collective-permute-start.1) | collective-permute-done | bytes 786464 | tf_op jit(solution)/shard_map/ppermute | solution.py:27
  33.4 1.3 broadcast_select_fusion.3
  34.7 1.3 pad_maximum_fusion
  36.1 1.2 collective-permute-start.2
  37.3 35.3 %collective-permute-done.2 = bf16[4,384,512]{1,2,0:T(8,128)(2,1)} collective-permute-done((bf16[4,384,512]{1,2,0:T(8,128)(2,1)}, bf16[4,384,512]{1,2,0:T(8,128)(2,1)}, u32[]{:S(2)}, u32[]{:S(2)}) %collective-permute-start.2) | collective-permute-done | bytes 1572896 | tf_op jit(solution)/shard_map/ppermute | solution.py:27
  72.6 1.8 broadcast_select_fusion.1
  76.0 2.6 fusion.7
  78.5 90.1 %all-gather.6.cloned.1.call-done = bf16[4096,2312]{1,0:T(8,128)(2,1)} async-done(((bf16[128,2312]{1,0:T(8,128)(2,1)}), bf16[4096,2312]{1,0:T(8,128)(2,1)}) %all-gather.6.cloned.1.call-update) | async-done | bytes 18939920 | tf_op jit(solution)/shard_map/all_gather | solution.py:39
  168.6 2.7 compare_select_fusion
  172.4 3.7 %fusion.28 = bf16[384,256]{1,0:T(8,128)(2,1)S(1)} fusion(bf16[384,4096]{0,1:T(8,128)(2,1)} %fusion.7, bf16[4096,2312]{1,0:T(8,128)(2,1)} %all-gather.6.cloned.1.call-done), kind=kOutput, calls=%fused_computation.41 | convolution fusion | flops 805404672 | bytes 5439488 | tf_op jit(solution)/shard_map/dot_general | solution.py:150
  176.1 1.4 collective-permute-start.4
  177.6 6.0 %fusion.22 = bf16[384,1024]{1,0:T(8,128)(2,1)S(1)} fusion(bf16[384,4096]{0,1:T(8,128)(2,1)S(1)} %copy-done.1, bf16[4096,2312]{1,0:T(8,128)(2,1)} %all-gather.6.cloned.1.call-done), kind=kOutput, calls=%fused_computation.39 | convolution fusion | flops 3221618688 | bytes 12320768 | tf_op jit(solution)/shard_map/dot_general | solution.py:148
  183.6 3.2 collective-permute-start.3
  188.4 2.2 convert_bitcast_fusion
  191.4 1.3 convolution_bitcast_fusion
  192.7 3.0 while.13
  198.1 13.2 %all-reduce = f32[64]{0:T(128)S(1)} all-reduce(f32[64]{0:T(128)S(1)} %exponential_dynamic-update-slice_fusion), channel_id=2, replica_groups=mesh['seq_0'=4,'seq_1'=8,'tensor'=8] {'seq_1'}, use_global_device_ids=true, to_apply=%add | all-reduce | flops 64 | bytes 512
  212.0 41.1 %all-gather.10.cloned.1.call-done = f32[8,8,128,128]{3,2,1,0:T(8,128)} async-done(((f32[1,8,128,128]{3,2,1,0:T(8,128)}), f32[8,8,128,128]{3,2,1,0:T(8,128)}) %all-gather.10.cloned.1.call-update) | async-done | bytes 4194320 | tf_op jit(solution)/shard_map/all_gather | solution.py:61
  253.1 3.5 fusion.53
  257.3 7.7 %all_gather.23 = f32[4,1,8]{2,1,0:T(1,128)S(1)} all-gather(f32[1,1,8]{2,1,0:T(1,128)S(1)} %get-tuple-element.116), channel_id=1, replica_groups=mesh['seq_0'=4,'seq_1'=8,'tensor'=8] {'seq_0'}, dimensions={0}, use_global_device_ids=true | all-gather | bytes 160 | tf_op jit(solution)/shard_map/all_gather | solution.py:61
  268.3 3.3 fusion.34
  271.6 17.0 %all-gather.8.cloned.1.call-done = f32[4,1,8,128,128]{4,3,2,1,0:T(8,128)} async-done(((f32[1,1,8,128,128]{4,3,2,1,0:T(8,128)}), f32[4,1,8,128,128]{4,3,2,1,0:T(8,128)}) %all-gather.8.cloned.1.call-update) | async-done | bytes 2097168 | tf_op jit(solution)/shard_map/all_gather | solution.py:61
  288.7 3.7 %fusion.52 = f32[8,128,128]{2,1,0:T(8,128)S(1)} fusion(f32[4,1,8,128,128]{4,3,2,1,0:T(8,128)} %all-gather.8.cloned.1.call-done, f32[1,1,8,128,128]{4,3,2,1,0:T(8,128)S(1)} %copy-done.4, f32[1,1,8,128,128]{4,3,2,1,0:T(8,128)S(1)} %copy-done.6, f32[8,8,128,128]{3,2,1,0:T(8,128)} %all-gather.10.cloned.1.call-done, f32[8]{0:T(128)S(1)} %copy-done.24, ...), kind=kLoop, calls=%fused_computation.71 | loop fusion | flops 4194304 | bytes 6816108 | tf_op jit(solution)/shard_map/mul | solution.py:189
  292.5 1.7 fusion.15
  294.2 3.2 copy.64
  297.4 7.9 %multiply_reduce_fusion.1 = (f32[384]{0:T(512)S(1)}, f32[384,1024]{1,0:T(8,128)S(1)}) fusion(bf16[384,4096]{0,1:T(8,128)(2,1)S(1)} %copy-done.2, bf16[4096,2312]{1,0:T(8,128)(2,1)} %all-gather.6.cloned.1.call-done, f32[48,8,8,128]{3,2,1,0:T(8,128)} %bitcast.206), kind=kOutput, calls=%fused_computation.30 | convolution fusion | flops 3224763904 | bytes 14681600 | tf_op jit(solution)/shard_map/dot_general | solution.py:149
  305.3 8.8 %fusion.37 = f32[384,4096]{1,0:T(8,128)} fusion(bf16[1024,4096]{1,0:T(8,128)(2,1)} %param.31, f32[384,1024]{1,0:T(8,128)S(1)} %get-tuple-element.123, f32[1024]{0:T(1024)S(1)} %copy-done.40, f32[384]{0:T(512)S(1)} %add_rsqrt_fusion), kind=kOutput, calls=%fused_computation.49 | convolution fusion | flops 3222405120 | bytes 16258560 | tf_op jit(solution)/shard_map/dot_general | solution.py:204
  314.2 44.9 %reduce-scatter.2.cloned.1.call-done = f32[384,512]{1,0:T(8,128)} async-done(((f32[384,4096]{1,0:T(8,128)}), f32[384,512]{1,0:T(8,128)}) %reduce-scatter.2.cloned.1.call-update) | async-done | bytes 786448 | tf_op jit(solution)/shard_map/reduce_scatter | solution.py:205
  359.1 2.0 add_convert_fusion
  (142 shorter events, 15.2 us)
Async XLA Ops:
  6.5 162.0 %all-gather.6.cloned.1.call-start = ((), (), s32[]{:S(2)}) async-start(), calls=%async_computation.1 | async-start | bytes 20545536 | tf_op jit(solution)/shard_map/all_gather | solution.py:39
  9.4 243.7 %all-gather.10.cloned.1.call-start = ((), (), s32[]{:S(2)}) async-start(), calls=%async_computation.4 | async-start | bytes 4718592 | tf_op jit(solution)/shard_map/all_gather | solution.py:61
  9.6 4.6 %collective-permute-start = (bf16[1,384,512]{1,2,0:T(8,128)(2,1)S(1)}, bf16[1,384,512]{1,2,0:T(8,128)(2,1)S(1)}, u32[]{:S(2)}, u32[]{:S(2)}) collective-permute-start(bf16[1,384,512]{1,2,0:T(8,128)(2,1)S(1)} %bitcast.207), channel_id=1, source_target_pairs={{0,1},{1,0},{2,3},{3,2},{4,5},{5,4},{6,7},{7,6},{8,9},{9,8},{10,11... | collective-permute-start | bytes 1179656 | tf_op jit(solution)/shard_map/ppermute | solution.py:27
  14.4 18.9 %collective-permute-start.1 = (bf16[2,384,512]{1,2,0:T(8,128)(2,1)S(1)}, bf16[2,384,512]{1,2,0:T(8,128)(2,1)}, u32[]{:S(2)}, u32[]{:S(2)}) collective-permute-start(bf16[2,384,512]{1,2,0:T(8,128)(2,1)S(1)} %pad_maximum_fusion.2), channel_id=1, source_target_pairs={{0,2},{1,3},{2,0},{3,1},{4,6},{5,7},{6,4},{7,5},{8,10},{9,11},{10,... | collective-permute-start | bytes 2359304 | tf_op jit(solution)/shard_map/ppermute | solution.py:27
  36.1 36.6 %collective-permute-start.2 = (bf16[4,384,512]{1,2,0:T(8,128)(2,1)}, bf16[4,384,512]{1,2,0:T(8,128)(2,1)}, u32[]{:S(2)}, u32[]{:S(2)}) collective-permute-start(bf16[4,384,512]{1,2,0:T(8,128)(2,1)} %pad_maximum_fusion), channel_id=1, source_target_pairs={{0,4},{1,5},{2,6},{3,7},{4,0},{5,1},{6,2},{7,3},{8,12},{9,13},{10,... | collective-permute-start | bytes 4718600 | tf_op jit(solution)/shard_map/ppermute | solution.py:27
  76.0 92.6 %copy-start.16 = (f32[8]{0:T(128)S(1)}, f32[8]{0:T(128)}, u32[]{:S(2)}) copy-start(f32[8]{0:T(128)} %param.23) | copy-start | bytes 100
  78.5 92.8 %copy-start.38 = (f32[8]{0:T(128)S(1)}, f32[8]{0:T(128)}, u32[]{:S(2)}) copy-start(f32[8]{0:T(128)} %param.24) | copy-start | bytes 100
  176.1 11.3 %collective-permute-start.4 = (bf16[3,1,256]{2,0,1:T(4,128)(2,1)S(1)}, bf16[3,1,256]{2,0,1:T(4,128)(2,1)S(1)}, u32[]{:S(2)}, u32[]{:S(2)}) collective-permute-start(bf16[3,1,256]{2,0,1:T(4,128)(2,1)S(1)} %slice_bitcast_fusion.8), channel_id=1, source_target_pairs={{0,8},{8,16},{16,24},{24,32},{32,40},{40,48},{48,56},{56,64},{64,7... | collective-permute-start | bytes 4616 | tf_op jit(solution)/shard_map/ppermute | solution.py:47
  183.6 4.8 %collective-permute-start.3 = (bf16[3,1024]{1,0:T(4,128)(2,1)S(1)}, bf16[3,1024]{1,0:T(4,128)(2,1)S(1)}, u32[]{:S(2)}, u32[]{:S(2)}) collective-permute-start(bf16[3,1024]{1,0:T(4,128)(2,1)S(1)} %slice.193), channel_id=1, source_target_pairs={{0,8},{8,16},{16,24},{24,32},{32,40},{40,48},{48,56},{56,64},{64,7... | collective-permute-start | bytes 18440 | tf_op jit(solution)/shard_map/ppermute | solution.py:47
  196.5 92.1 %all-gather.8.cloned.1.call-start = ((), (), s32[]{:S(2)}) async-start(), calls=%async_computation.2 | async-start | bytes 2621440 | tf_op jit(solution)/shard_map/all_gather | solution.py:61
  211.4 45.2 %copy-start.17 = (f32[8]{0:T(128)}, f32[8]{0:T(128)S(1)}, u32[]{:S(2)}) copy-start(f32[8]{0:T(128)S(1)} %get-tuple-element.118) | copy-start | bytes 100
  211.4 45.2 %copy-start.19 = (f32[8]{0:T(128)}, f32[8]{0:T(128)S(1)}, u32[]{:S(2)}) copy-start(f32[8]{0:T(128)S(1)} %get-tuple-element.119) | copy-start | bytes 100
  211.4 45.2 %copy-start.21 = (f32[8]{0:T(128)}, f32[8]{0:T(128)S(1)}, u32[]{:S(2)}) copy-start(f32[8]{0:T(128)S(1)} %get-tuple-element.121) | copy-start | bytes 100
  212.0 44.6 %copy-start.23 = (f32[8]{0:T(128)}, f32[8]{0:T(128)S(1)}, u32[]{:S(2)}) copy-start(f32[8]{0:T(128)S(1)} %get-tuple-element.113) | copy-start | bytes 100
  212.0 44.6 %copy-start.25 = (f32[8]{0:T(128)}, f32[8]{0:T(128)S(1)}, u32[]{:S(2)}) copy-start(f32[8]{0:T(128)S(1)} %get-tuple-element.114) | copy-start | bytes 100
  212.0 44.7 %copy-start.27 = (f32[8]{0:T(128)}, f32[8]{0:T(128)S(1)}, u32[]{:S(2)}) copy-start(f32[8]{0:T(128)S(1)} %get-tuple-element.115) | copy-start | bytes 100
  253.1 13.3 %copy-start.11 = (bf16[384,1,128]{2,0,1:T(8,128)(2,1)S(1)}, bf16[384,1,128]{2,0,1:T(8,128)(2,1)}, u32[]{:S(2)}) copy-start(bf16[384,1,128]{2,0,1:T(8,128)(2,1)} %get-tuple-element.97) | copy-start | bytes 294916
  253.1 14.2 %copy-start.3 = (f32[48,8,8,128]{3,1,2,0:T(8,128)S(1)}, f32[48,8,8,128]{3,1,2,0:T(8,128)}, u32[]{:S(2)}) copy-start(f32[48,8,8,128]{3,1,2,0:T(8,128)} %get-tuple-element.85) | copy-start | bytes 4718596
  256.7 102.4 %reduce-scatter.2.cloned.1.call-start = ((), (), s32[]{:S(2)}) async-start(), calls=%async_computation.3 | async-start | bytes 7077888 | tf_op jit(solution)/shard_map/reduce_scatter | solution.py:205
  268.1 20.5 %copy-start.4 = (f32[1,1,8,128,128]{4,3,2,1,0:T(8,128)S(1)}, f32[1,1,8,128,128]{4,3,2,1,0:T(8,128)}, u32[]{:S(2)}) copy-start(f32[1,1,8,128,128]{4,3,2,1,0:T(8,128)} %get-tuple-element.83) | copy-start | bytes 1572868
  268.1 20.5 %copy-start.6 = (f32[1,1,8,128,128]{4,3,2,1,0:T(8,128)S(1)}, f32[1,1,8,128,128]{4,3,2,1,0:T(8,128)}, u32[]{:S(2)}) copy-start(f32[1,1,8,128,128]{4,3,2,1,0:T(8,128)} %get-tuple-element.84) | copy-start | bytes 1572868
  268.1 20.5 %copy-start.18 = (f32[8]{0:T(128)S(1)}, f32[8]{0:T(128)}, u32[]{:S(2)}) copy-start(f32[8]{0:T(128)} %copy-done.17) | copy-start | bytes 100
  268.2 20.4 %copy-start.20 = (f32[8]{0:T(128)S(1)}, f32[8]{0:T(128)}, u32[]{:S(2)}) copy-start(f32[8]{0:T(128)} %copy-done.19) | copy-start | bytes 100
  268.2 20.4 %copy-start.22 = (f32[8]{0:T(128)S(1)}, f32[8]{0:T(128)}, u32[]{:S(2)}) copy-start(f32[8]{0:T(128)} %copy-done.21) | copy-start | bytes 100
  268.2 20.4 %copy-start.24 = (f32[8]{0:T(128)S(1)}, f32[8]{0:T(128)}, u32[]{:S(2)}) copy-start(f32[8]{0:T(128)} %copy-done.23) | copy-start | bytes 100
  268.2 20.4 %copy-start.26 = (f32[8]{0:T(128)S(1)}, f32[8]{0:T(128)}, u32[]{:S(2)}) copy-start(f32[8]{0:T(128)} %copy-done.25) | copy-start | bytes 100
  268.2 20.4 %copy-start.28 = (f32[8]{0:T(128)S(1)}, f32[8]{0:T(128)}, u32[]{:S(2)}) copy-start(f32[8]{0:T(128)} %copy-done.27) | copy-start | bytes 100
  268.2 20.4 %copy-start.31 = (f32[8]{0:T(128)S(1)}, f32[8]{0:T(128)}, u32[]{:S(2)}) copy-start(f32[8]{0:T(128)} %get-tuple-element.112) | copy-start | bytes 100
  268.2 20.4 %copy-start.32 = (f32[8]{0:T(128)S(1)}, f32[8]{0:T(128)}, u32[]{:S(2)}) copy-start(f32[8]{0:T(128)} %get-tuple-element.108) | copy-start | bytes 100
  268.2 20.4 %copy-start.33 = (f32[8]{0:T(128)S(1)}, f32[8]{0:T(128)}, u32[]{:S(2)}) copy-start(f32[8]{0:T(128)} %get-tuple-element.109) | copy-start | bytes 100
  268.2 20.4 %copy-start.34 = (f32[8]{0:T(128)S(1)}, f32[8]{0:T(128)}, u32[]{:S(2)}) copy-start(f32[8]{0:T(128)} %get-tuple-element.110) | copy-start | bytes 100
  268.2 20.4 %copy-start.35 = (f32[8]{0:T(128)S(1)}, f32[8]{0:T(128)}, u32[]{:S(2)}) copy-start(f32[8]{0:T(128)} %get-tuple-element.111) | copy-start | bytes 100
  (19 other events, 92.3 us)
Sparse Core Ops, SparseCore 0:
  9.9 158.6 all-gather.5
  196.6 56.3 all-gather.9
  256.8 31.7 all-gather.7
  314.3 44.7 reduce-scatter.1
